TPU v7x, 32 devices: a whole 2x2x4 slice. The times are simulated.
32 devices in a mesh: groups: 2 (over y), dp: 4 (over z), mp: 4 (over x, core).
Axes of the slice: x: 2, y: 2, z: 4, core: 2. Of those that a mesh axis runs over, the one named last changes fastest.
Arguments:
- tokens: bfloat16 [1024, 7168], P(('groups', 'dp')), parts along dimension 0, may hold values from -20 to 20, as said below
- w_down: bfloat16 [7168, 1536], P('dp', 'mp'), may hold values from -3 to 3, as said below
- gain: float32 [1536], P('mp'), may hold values from 0.25 to 1.75
- w_up: bfloat16 [1536, 26112], P('dp', 'mp'), may hold values from -0.15625 to 0.15625
- head_counts: int32 [4], replicated, may hold values from 30 to 34, as said below
- cotangent: bfloat16 [1024, 26112], P(('groups', 'dp'), 'mp'), parts along dimension 0, may hold values from -6 to 6
Outputs:
- queries: bfloat16 [1024, 26112], P(('groups', 'dp'), 'mp'), parts along dimension 0
- grad_tokens: bfloat16 [1024, 7168], P(('groups', 'dp'), 'mp'), parts along dimension 0
There are 2 independent parts, one for each index of `groups`. A program takes and returns all parts, laid end to end along the dimension named above; an argument that names none is the same for every part. Nothing has to cross between parts.
Inputs may be any that keep to these rules, and one draw needn't show every extreme that they name: `tokens`: hidden states of order one with token scales that differ. `w_down`: entries of order 7168^(-1/2). `head_counts`: the entries sum to 128; one of them is 34.
All inputs are finite; a program needn't handle non-finite values.
Results may differ from a plain program's by a relative error of at most 0.018.
Values may be sent and summed in bfloat16 or wider, within the bound.
A program may use at most 128 MiB of HBM per device.

v0:
```python
import jax
import jax.numpy as jnp
from jax import lax
from jax.sharding import PartitionSpec as P

HD = 192


def contract_last(left, right):
    return lax.dot_general(
        left, right, (((1,), (1,)), ((), ())), preferred_element_type=jnp.float32
    )


def body(tokens, w_down, gain, w_up, head_counts, cotangent):
    block_cols = w_up.shape[1]
    latent_width = w_down.shape[1] * lax.axis_size("mp")
    position = lax.axis_index("mp")
    held_heads = lax.dynamic_slice_in_dim(head_counts, position, 1, 0)
    slot_index = jnp.arange(block_cols, dtype=jnp.int32) // HD
    keep_mask = (slot_index < held_heads).astype(jnp.float32)
    down_whole = lax.all_gather(w_down, "dp", axis=0, tiled=True)
    latent_raw = jnp.dot(tokens, down_whole, preferred_element_type=jnp.float32)
    squares = lax.psum(jnp.sum(latent_raw * latent_raw, axis=1, keepdims=True), "mp")
    root_mean = jnp.sqrt(squares / latent_width + 1e-06)
    latent_local = (latent_raw / root_mean * gain).astype(jnp.bfloat16)
    latent = lax.all_gather(latent_local, "mp", axis=1, tiled=True)
    masked = cotangent * keep_mask.astype(jnp.bfloat16)
    up_whole = lax.all_gather(w_up, "dp", axis=0, tiled=True)
    query_total = jnp.dot(latent, up_whole, preferred_element_type=jnp.float32)
    grad_partial = contract_last(masked, up_whole)
    queries = (query_total * keep_mask).astype(jnp.bfloat16)
    grad_latent = lax.psum_scatter(
        grad_partial.astype(jnp.bfloat16), "mp", scatter_dimension=1, tiled=True
    ).astype(jnp.float32)
    inner_dot = lax.psum(jnp.sum(gain * grad_latent * latent_raw, axis=1, keepdims=True), "mp")
    grad_raw = (
        gain * grad_latent / root_mean - latent_raw * inner_dot / (latent_width * root_mean**3)
    ).astype(jnp.bfloat16)
    partial_value = contract_last(grad_raw, down_whole).astype(jnp.bfloat16).astype(jnp.float32)
    grad_tokens = lax.psum_scatter(
        partial_value.astype(jnp.bfloat16), "mp", scatter_dimension=1, tiled=True
    )
    return (queries, grad_tokens)


def solution(mesh):
    in_specs = (
        P(("groups", "dp"), None),
        P("dp", "mp"),
        P("mp"),
        P("dp", "mp"),
        P(),
        P(("groups", "dp"), "mp"),
    )
    out_specs = (P(("groups", "dp"), "mp"), P(("groups", "dp"), "mp"))
    return jax.shard_map(body, mesh=mesh, in_specs=in_specs, out_specs=out_specs, check_vma=False)
```

profile of v0, /device:TPU:2, one launch (start us, length us, event | category | flops | bytes accessed | tf_op | source)
XLA Modules:
  0.0 538.7 jit_solution(8078092446914638114)
XLA Ops:
  7.2 0.0 copy-start
  7.2 0.0 copy-start.3
  7.2 0.0 copy-start.1
  7.2 0.0 all-gather.5.cloned.1.call-start
  7.2 0.7 all-gather.5.cloned.1.call-update
  7.9 0.0 reduce-scatter.7.cloned.1.call-start
  8.0 0.0 copy-done.3
  8.0 0.6 dynamic_slice.3
  8.6 0.6 fusion.12
  9.1 0.0 copy-start.2
  9.1 343.6 %all-gather.5.cloned.1.call-done = bf16[1536,6528]{1,0:T(8,128)(2,1)} async-done(((bf16[384,6528]{1,0:T(8,128)(2,1)}), bf16[1536,6528]{1,0:T(8,128)(2,1)}) %all-gather.5.cloned.1.call-update) | async-done | bytes 20054032 | tf_op jit(solution)/shard_map/all_gather | solution.py:29
  352.7 0.0 copy-done.1
  352.7 11.5 %convolution_convert_fusion.1 = bf16[128,1536]{1,0:T(8,128)(2,1)} fusion(bf16[1536,6528]{1,0:T(8,128)(2,1)} %all-gather.5.cloned.1.call-done, bf16[128,6528]{1,0:T(8,128)(2,1)S(1)} %copy-done.1, bf16[6528]{0:T(1024)(128)(2,1)S(1)} %fusion.12), kind=kOutput, calls=%fused_computation.3 | convolution fusion | flops 2567946240 | bytes 22131456 | tf_op jit(solution)/shard_map/dot_general | solution.py:10
  364.2 1.9 copy.8
  366.1 0.0 reduce-scatter.7.cloned.1.call-update
  366.1 0.0 all-gather.3.cloned.1.call-start
  366.2 0.7 all-gather.3.cloned.1.call-update
  366.8 0.0 reduce-scatter.5.cloned.1.call-start
  366.9 17.8 %reduce-scatter.7.cloned.1.call-done = bf16[384,128]{1,0:T(8,128)(2,1)} async-done(((bf16[1536,128]{1,0:T(8,128)(2,1)}), bf16[384,128]{1,0:T(8,128)(2,1)}) %reduce-scatter.7.cloned.1.call-update) | async-done | bytes 98320
  384.6 1.0 copy.9
  385.6 104.1 %all-gather.3.cloned.1.call-done = bf16[7168,384]{1,0:T(8,128)(2,1)} async-done(((bf16[1792,384]{1,0:T(8,128)(2,1)}), bf16[7168,384]{1,0:T(8,128)(2,1)}) %all-gather.3.cloned.1.call-update) | async-done | bytes 5505040 | tf_op jit(solution)/shard_map/all_gather | solution.py:22
  489.7 0.0 copy-done
  489.7 0.0 copy-done.2
  489.7 3.8 multiply_reduce_fusion
  493.5 5.9 %all-reduce = (f32[128,1]{0,1:T(1,128)S(1)}, f32[128]{0:T(128)S(1)}) all-reduce(f32[128,1]{0,1:T(1,128)S(1)} %bitcast.16, f32[128]{0:T(128)S(1)} %get-tuple-element.2), channel_id=1, replica_groups=mesh['groups'=2,'dp'=4,'mp'=4] {'mp'}, use_global_device_ids=true, to_apply=%region_1.2 | all-reduce | flops 256 | bytes 2048 | tf_op jit(solution)/shard_map/psum | solution.py:24
  499.5 5.7 %convolution_convert_fusion = bf16[128,7168]{1,0:T(8,128)(2,1)} fusion(bf16[7168,384]{1,0:T(8,128)(2,1)} %all-gather.3.cloned.1.call-done, f32[128,384]{1,0:T(8,128)S(1)} %get-tuple-element.8, bf16[128,384]{1,0:T(8,128)(2,1)S(1)} %copy.9, f32[128]{0:T(128)S(1)} %get-tuple-element.6, f32[128]{0:T(128)S(1)} %get-tuple-element.5, f32[384]{0:T(512)S(1)} %copy-done.2, ...), kind=kOutput, calls=%fused_computation.2 | convolution fusion | flops 705904640 | bytes 7638016 | tf_op jit(solution)/shard_map/dot_general | solution.py:10
  505.1 0.0 reduce-scatter.5.cloned.1.call-update
  505.1 0.6 fusion.10
  505.7 0.1 multiply_convert_fusion
  505.8 6.5 %all_gather.10 = bf16[128,1536]{1,0:T(8,128)(2,1)S(1)} all-gather(bf16[128,384]{1,0:T(8,128)(2,1)S(1)} %multiply_convert_fusion), channel_id=1, replica_groups=mesh['groups'=2,'dp'=4,'mp'=4] {'mp'}, dimensions={1}, use_global_device_ids=true | all-gather | bytes 491520 | tf_op jit(solution)/shard_map/all_gather | solution.py:27
  512.3 10.8 %fusion = bf16[128,6528]{1,0:T(8,128)(2,1)} fusion(bf16[128,1536]{1,0:T(8,128)(2,1)S(1)} %all_gather.10, bf16[1536,6528]{1,0:T(8,128)(2,1)} %all-gather.5.cloned.1.call-done, f32[6528]{0:T(1024)S(1)} %fusion.10), kind=kOutput, calls=%fused_computation.1 | convolution fusion | flops 2568585216 | bytes 22144512 | tf_op jit(solution)/shard_map/dot_general | solution.py:30
  523.1 9.1 %reduce-scatter.5.cloned.1.call-done = bf16[128,1792]{1,0:T(8,128)(2,1)} async-done(((bf16[128,7168]{1,0:T(8,128)(2,1)}), bf16[128,1792]{1,0:T(8,128)(2,1)}) %reduce-scatter.5.cloned.1.call-update) | async-done | bytes 458768 | tf_op jit(solution)/shard_map/reduce_scatter | solution.py:41
  (1 shorter events, 0.0 us)
Async XLA Ops:
  7.2 482.6 %copy-start = (bf16[128,7168]{1,0:T(8,128)(2,1)S(1)}, bf16[128,7168]{1,0:T(8,128)(2,1)}, u32[]{:S(2)}) copy-start(bf16[128,7168]{1,0:T(8,128)(2,1)} %param.6) | copy-start | bytes 5505028
  7.2 0.8 copy-start.3
  7.2 345.5 %copy-start.1 = (bf16[128,6528]{1,0:T(8,128)(2,1)S(1)}, bf16[128,6528]{1,0:T(8,128)(2,1)}, u32[]{:S(2)}) copy-start(bf16[128,6528]{1,0:T(8,128)(2,1)} %param.11) | copy-start | bytes 5013508
  7.2 345.5 %all-gather.5.cloned.1.call-start = ((), (), s32[]{:S(2)}) async-start(), calls=%async_computation.3 | async-start | bytes 25067520 | tf_op jit(solution)/shard_map/all_gather | solution.py:29
  7.9 376.7 %reduce-scatter.7.cloned.1.call-start = ((), (), s32[]{:S(2)}) async-start(), calls=%async_computation.5 | async-start | bytes 491520
  9.1 480.6 %copy-start.2 = (f32[384]{0:T(512)S(1)}, f32[384]{0:T(512)}, u32[]{:S(2)}) copy-start(f32[384]{0:T(512)} %param.8) | copy-start | bytes 4612
  366.1 123.6 %all-gather.3.cloned.1.call-start = ((), (), s32[]{:S(2)}) async-start(), calls=%async_computation.2 | async-start | bytes 6881280 | tf_op jit(solution)/shard_map/all_gather | solution.py:22
  366.8 165.3 %reduce-scatter.5.cloned.1.call-start = ((), (), s32[]{:S(2)}) async-start(), calls=%async_computation.4 | async-start | bytes 2293760 | tf_op jit(solution)/shard_map/reduce_scatter | solution.py:41
Sparse Core Ops, SparseCore 0:
  9.6 343.0 all-gather.4
  366.2 18.3 reduce-scatter.6
  386.2 103.4 all-gather.2
  505.3 26.8 reduce-scatter.4
where the time goes:
time: 542 us; the launch traced here: 539 us
  waiting for transfers between devices  476 us (88%)
  matrix products  31.7 us (6%)
  between operations  13.8 us (3%)
  blocking collectives  12.4 us (2%)
    all_gather x1, waiting for transfers between devices, body(): up_whole = lax.all_gather(w_up, 'dp', axis=0, tiled=True)  344 us
    all_gather x1, waiting for transfers between devices, body(): down_whole = lax.all_gather(w_down, 'dp', axis=0, tiled=True)  104 us
    unnamed x5, waiting for transfers between devices  19.1 us
    dot_general x2, matrix products, contract_last(): lax.dot_general(left, right, (((1,), (1,)), ((), ())), preferred_element_...  17.1 us
  transfers between devices with their start and end apart: 4, of which 4 were waited for; matrix products, arithmetic and copies ran while one was open for 3% of the time, Pallas kernels for 0%

commit v1 on v0

--- a/solution.py
+++ b/solution.py
@@ -12,13 +12,16 @@
     )
 
 
-def body(tokens, w_down, gain, w_up, head_counts, cotangent):
-    block_cols = w_up.shape[1]
-    latent_width = w_down.shape[1] * lax.axis_size("mp")
+def keep_mask_of(head_counts, block_cols):
     position = lax.axis_index("mp")
     held_heads = lax.dynamic_slice_in_dim(head_counts, position, 1, 0)
     slot_index = jnp.arange(block_cols, dtype=jnp.int32) // HD
-    keep_mask = (slot_index < held_heads).astype(jnp.float32)
+    return (slot_index < held_heads).astype(jnp.float32)
+
+
+def gather_weights_body(tokens, w_down, gain, w_up, head_counts, cotangent):
+    latent_width = w_down.shape[1] * lax.axis_size("mp")
+    keep_mask = keep_mask_of(head_counts, w_up.shape[1])
     down_whole = lax.all_gather(w_down, "dp", axis=0, tiled=True)
     latent_raw = jnp.dot(tokens, down_whole, preferred_element_type=jnp.float32)
     squares = lax.psum(jnp.sum(latent_raw * latent_raw, axis=1, keepdims=True), "mp")
@@ -37,9 +40,48 @@
     grad_raw = (
         gain * grad_latent / root_mean - latent_raw * inner_dot / (latent_width * root_mean**3)
     ).astype(jnp.bfloat16)
-    partial_value = contract_last(grad_raw, down_whole).astype(jnp.bfloat16).astype(jnp.float32)
-    grad_tokens = lax.psum_scatter(
-        partial_value.astype(jnp.bfloat16), "mp", scatter_dimension=1, tiled=True
+    partial_value = contract_last(grad_raw, down_whole).astype(jnp.bfloat16)
+    grad_tokens = lax.psum_scatter(partial_value, "mp", scatter_dimension=1, tiled=True)
+    return (queries, grad_tokens)
+
+
+def move_tokens_body(tokens, w_down, gain, w_up, head_counts, cotangent):
+    n = lax.axis_size("mp")
+    swap = [(i * n + j, j * n + i) for i in range(n) for j in range(n)]
+    position = lax.axis_index("mp")
+    latent_width = w_down.shape[1] * n
+    keep_mask = keep_mask_of(head_counts, w_up.shape[1])
+
+    def transpose_owner(block):
+        return lax.ppermute(block, ("dp", "mp"), swap)
+
+    rows = w_down.shape[0]
+    tokens_block = lax.dynamic_slice_in_dim(tokens, position * rows, rows, 1)
+    tokens_cols = lax.all_gather(transpose_owner(tokens_block), "mp", axis=0, tiled=True)
+    raw_partial = jnp.dot(tokens_cols, w_down, preferred_element_type=jnp.float32)
+    latent_raw = lax.psum_scatter(raw_partial, "dp", scatter_dimension=0, tiled=True)
+    squares = lax.psum(jnp.sum(latent_raw * latent_raw, axis=1, keepdims=True), "mp")
+    root_mean = jnp.sqrt(squares / latent_width + 1e-06)
+    latent_local = (latent_raw / root_mean * gain).astype(jnp.bfloat16)
+    latent = lax.all_gather(transpose_owner(latent_local), "mp", axis=0, tiled=True)
+    query_partial = (
+        jnp.dot(latent, w_up, preferred_element_type=jnp.float32) * keep_mask
+    ).astype(jnp.bfloat16)
+    masked = cotangent * keep_mask.astype(jnp.bfloat16)
+    masked_all = lax.all_gather(masked, "dp", axis=0, tiled=True)
+    queries = lax.psum_scatter(query_partial, "dp", scatter_dimension=0, tiled=True)
+    grad_partial = contract_last(masked_all, w_up).astype(jnp.bfloat16)
+    grad_latent = transpose_owner(
+        lax.psum_scatter(grad_partial, "mp", scatter_dimension=0, tiled=True)
+    ).astype(jnp.float32)
+    inner_dot = lax.psum(jnp.sum(gain * grad_latent * latent_raw, axis=1, keepdims=True), "mp")
+    grad_raw = (
+        gain * grad_latent / root_mean - latent_raw * inner_dot / (latent_width * root_mean**3)
+    ).astype(jnp.bfloat16)
+    grad_raw_all = lax.all_gather(grad_raw, "dp", axis=0, tiled=True)
+    token_partial = contract_last(grad_raw_all, w_down).astype(jnp.bfloat16)
+    grad_tokens = transpose_owner(
+        lax.psum_scatter(token_partial, "mp", scatter_dimension=0, tiled=True)
     )
     return (queries, grad_tokens)
 
@@ -54,4 +96,6 @@
         P(("groups", "dp"), "mp"),
     )
     out_specs = (P(("groups", "dp"), "mp"), P(("groups", "dp"), "mp"))
+    square = mesh.shape["dp"] == mesh.shape["mp"]
+    body = move_tokens_body if square else gather_weights_body
     return jax.shard_map(body, mesh=mesh, in_specs=in_specs, out_specs=out_specs, check_vma=False)

time: 542 us -> 415 us (0.77)
  the two profiles are of different devices: /device:TPU:2 before, /device:TPU:9 now
where the time goes in v1:
time: 415 us
  waiting for transfers between devices  329 us (79%)
  blocking collectives  34.6 us (8%)
  matrix products  22.7 us (5%)
  between operations  14.2 us (3%)
  other arithmetic  6.03 us (1%)
  starting transfers between devices  4.8 us (1%)
    reduce_scatter x1, waiting for transfers between devices, move_tokens_body(): lax.psum_scatter(query_partial, 'dp', scatter_dimension=0, tiled=True)  133 us
    all_gather x1, waiting for transfers between devices, move_tokens_body(): masked_all = lax.all_gather(masked, 'dp', axis=0, tiled=True)  118 us
    all_gather x1, waiting for transfers between devices, move_tokens_body(): lax.all_gather(transpose_owner(tokens_block), 'mp', axis=0, tiled=True)  28.4 us
    reduce_scatter x1, waiting for transfers between devices, move_tokens_body(): lax.psum_scatter(raw_partial, 'dp', scatter_dimension=0, tiled=True)  22.3 us
    reduce_scatter x1, waiting for transfers between devices, move_tokens_body(): lax.psum_scatter(grad_partial, 'mp', scatter_dimension=0, tiled=True)  19.2 us
    all_gather x1, blocking collectives, move_tokens_body(): lax.all_gather(transpose_owner(latent_local), 'mp', axis=0, tiled=True)  16.2 us
    all_gather x1, blocking collectives, move_tokens_body(): grad_raw_all = lax.all_gather(grad_raw, 'dp', axis=0, tiled=True)  12 us
    dot_general x2, matrix products, contract_last(): lax.dot_general(left, right, (((1,), (1,)), ((), ())), preferred_element_...  11.2 us
  transfers between devices with their start and end apart: 10, of which 6 were waited for; matrix products, arithmetic and copies ran while one was open for 5% of the time, Pallas kernels for 0%

profile of v1, /device:TPU:9, one launch (start us, length us, event | category | flops | bytes accessed | tf_op | source)
XLA Modules:
  0.0 414.5 jit_solution(11642540966179792071)
XLA Ops:
  7.2 0.0 copy-start
  7.2 0.0 all-gather.5.cloned.1.call-start
  7.2 1.3 dynamic_slice.7
  8.6 0.6 fusion.5
  9.1 2.8 broadcast_multiply_fusion
  11.9 0.0 all-gather.5.cloned.1.call-update
  11.9 0.0 all-gather.3.cloned.1.call-start
  12.0 0.0 copy-done
  12.1 0.7 collective-permute-start
  12.8 0.0 collective-permute-done
  12.8 0.0 copy-start.2
  12.8 0.8 copy-done.2
  13.5 0.0 all-gather.3.cloned.1.call-update
  13.6 0.0 copy-start.1
  13.6 0.0 reduce-scatter.9.cloned.1.call-start
  13.6 118.5 %all-gather.5.cloned.1.call-done = bf16[512,6528]{1,0:T(8,128)(2,1)} async-done(((bf16[128,6528]{1,0:T(8,128)(2,1)}), bf16[512,6528]{1,0:T(8,128)(2,1)}) %all-gather.5.cloned.1.call-update) | async-done | bytes 6684688 | tf_op jit(solution)/shard_map/all_gather | solution.py:71
  132.1 8.7 %convolution_convert_fusion.1 = bf16[512,384]{1,0:T(8,128)(2,1)} fusion(bf16[512,6528]{1,0:T(8,128)(2,1)} %all-gather.5.cloned.1.call-done, bf16[384,6528]{1,0:T(8,128)(2,1)} %param.9), kind=kOutput, calls=%fused_computation.2 | convolution fusion | flops 2567110656 | bytes 12091392 | tf_op jit(solution)/shard_map/dot_general | solution.py:10
  140.8 0.0 reduce-scatter.9.cloned.1.call-update
  140.8 0.0 copy-start.3
  140.9 0.0 reduce-scatter.5.cloned.1.call-start
  140.9 28.4 %all-gather.3.cloned.1.call-done = bf16[512,1792]{1,0:T(8,128)(2,1)} async-done(((bf16[128,1792]{1,0:T(8,128)(2,1)}), bf16[512,1792]{1,0:T(8,128)(2,1)}) %all-gather.3.cloned.1.call-update) | async-done | bytes 1835024 | tf_op jit(solution)/shard_map/all_gather | solution.py:60
  169.3 0.0 copy-done.1
  169.3 3.5 fusion.9
  172.8 0.0 reduce-scatter.5.cloned.1.call-update
  172.8 0.0 reduce-scatter.11.cloned.1.call-start
  172.9 19.2 %reduce-scatter.9.cloned.1.call-done = bf16[128,384]{1,0:T(8,128)(2,1)} async-done(((bf16[512,384]{1,0:T(8,128)(2,1)}), bf16[128,384]{1,0:T(8,128)(2,1)}) %reduce-scatter.9.cloned.1.call-update) | async-done | bytes 98320 | tf_op jit(solution)/shard_map/reduce_scatter | solution.py:75
  192.1 1.5 collective-permute-start.2
  193.7 22.3 %reduce-scatter.5.cloned.1.call-done = f32[128,384]{1,0:T(8,128)} async-done(((f32[512,384]{1,0:T(8,128)}), f32[128,384]{1,0:T(8,128)}) %reduce-scatter.5.cloned.1.call-update) | async-done | bytes 196624 | tf_op jit(solution)/shard_map/reduce_scatter | solution.py:62
  216.0 0.0 collective-permute-done.2
  216.0 0.0 copy-done.3
  216.0 1.0 multiply_reduce_fusion
  217.0 6.4 %all-reduce = (f32[128,1]{0,1:T(1,128)S(1)}, f32[128]{0:T(128)S(1)}) all-reduce(f32[128,1]{0,1:T(1,128)S(1)} %bitcast.14, f32[128]{0:T(128)S(1)} %get-tuple-element.2), channel_id=1, replica_groups=mesh['groups'=2,'dp'=4,'mp'=4] {'mp'}, use_global_device_ids=true, to_apply=%region_2.3 | all-reduce | flops 256 | bytes 2048 | tf_op jit(solution)/shard_map/psum | solution.py:63
  223.5 1.1 subtract_convert_fusion
  224.6 12.0 %all_gather.15 = bf16[512,384]{1,0:T(8,128)(2,1)S(1)} all-gather(bf16[128,384]{1,0:T(8,128)(2,1)S(1)} %get-tuple-element.6), channel_id=1, replica_groups=mesh['groups'=2,'dp'=4,'mp'=4] {'dp'}, dimensions={0}, use_global_device_ids=true | all-gather | bytes 491520 | tf_op jit(solution)/shard_map/all_gather | solution.py:81
  236.5 2.4 convolution_convert_fusion
  239.0 0.0 reduce-scatter.11.cloned.1.call-update
  239.0 0.0 reduce-scatter.7.cloned.1.call-start
  239.0 0.7 collective-permute-start.1
  239.7 0.6 fusion.3
  240.3 0.0 collective-permute-done.1
  240.3 16.2 %all_gather.13 = bf16[512,384]{1,0:T(8,128)(2,1)S(1)} all-gather(bf16[128,384]{1,0:T(8,128)(2,1)S(1)} %collective-permute-done.1), channel_id=1, replica_groups=mesh['groups'=2,'dp'=4,'mp'=4] {'mp'}, dimensions={0}, use_global_device_ids=true | all-gather | bytes 491520 | tf_op jit(solution)/shard_map/all_gather | solution.py:66
  256.4 8.0 %multiply_convert_fusion = bf16[512,6528]{1,0:T(8,128)(2,1)} fusion(bf16[512,384]{1,0:T(8,128)(2,1)S(1)} %all_gather.13, bf16[384,6528]{1,0:T(8,128)(2,1)} %param.9, f32[6528]{0:T(1024)S(1)} %fusion.3), kind=kOutput, calls=%fused_computation | convolution fusion | flops 2573598720 | bytes 12117504 | tf_op jit(solution)/shard_map/dot_general | solution.py:68
  264.5 0.0 reduce-scatter.7.cloned.1.call-update
  264.5 8.1 %reduce-scatter.11.cloned.1.call-done = bf16[128,1792]{1,0:T(8,128)(2,1)} async-done(((bf16[512,1792]{1,0:T(8,128)(2,1)}), bf16[128,1792]{1,0:T(8,128)(2,1)}) %reduce-scatter.11.cloned.1.call-update) | async-done | bytes 458768 | tf_op jit(solution)/shard_map/reduce_scatter | solution.py:84
  272.5 1.7 collective-permute-start.3
  274.2 0.0 collective-permute-done.3
  274.2 132.7 %reduce-scatter.7.cloned.1.call-done = bf16[128,6528]{1,0:T(8,128)(2,1)} async-done(((bf16[512,6528]{1,0:T(8,128)(2,1)}), bf16[128,6528]{1,0:T(8,128)(2,1)}) %reduce-scatter.7.cloned.1.call-update) | async-done | bytes 1671184 | tf_op jit(solution)/shard_map/reduce_scatter | solution.py:72
  406.9 0.8 copy.9
  (2 shorter events, 0.1 us)
Async XLA Ops:
  7.2 4.8 %copy-start = (bf16[128,7168]{1,0:T(8,128)(2,1)S(1)}, bf16[128,7168]{1,0:T(8,128)(2,1)}, u32[]{:S(2)}) copy-start(bf16[128,7168]{1,0:T(8,128)(2,1)} %param.6) | copy-start | bytes 5505028
  7.2 124.9 %all-gather.5.cloned.1.call-start = ((), (), s32[]{:S(2)}) async-start(), calls=%async_computation.7 | async-start | bytes 8355840 | tf_op jit(solution)/shard_map/all_gather | solution.py:71
  11.9 157.4 %all-gather.3.cloned.1.call-start = ((), (), s32[]{:S(2)}) async-start(), calls=%async_computation.4 | async-start | bytes 2293760 | tf_op jit(solution)/shard_map/all_gather | solution.py:60
  12.1 0.7 collective-permute-start
  12.8 0.8 copy-start.2
  13.6 155.8 %copy-start.1 = (bf16[1792,384]{1,0:T(8,128)(2,1)S(1)}, bf16[1792,384]{1,0:T(8,128)(2,1)}, u32[]{:S(2)}) copy-start(bf16[1792,384]{1,0:T(8,128)(2,1)} %param.7) | copy-start | bytes 4128772
  13.6 178.5 %reduce-scatter.9.cloned.1.call-start = ((), (), s32[]{:S(2)}) async-start(), calls=%async_computation.8 | async-start | bytes 491520 | tf_op jit(solution)/shard_map/reduce_scatter | solution.py:75
  140.8 75.2 %copy-start.3 = (f32[384]{0:T(512)S(1)}, f32[384]{0:T(512)}, u32[]{:S(2)}) copy-start(f32[384]{0:T(512)} %param.8) | copy-start | bytes 4612
  140.9 75.1 %reduce-scatter.5.cloned.1.call-start = ((), (), s32[]{:S(2)}) async-start(), calls=%async_computation.5 | async-start | bytes 983040 | tf_op jit(solution)/shard_map/reduce_scatter | solution.py:62
  172.8 99.7 %reduce-scatter.11.cloned.1.call-start = ((), (), s32[]{:S(2)}) async-start(), calls=%async_computation.9 | async-start | bytes 2293760 | tf_op jit(solution)/shard_map/reduce_scatter | solution.py:84
  192.1 23.9 %collective-permute-start.2 = (bf16[128,384]{1,0:T(8,128)(2,1)}, bf16[128,384]{1,0:T(8,128)(2,1)S(1)}, u32[]{:S(2)}, u32[]{:S(2)}) collective-permute-start(bf16[128,384]{1,0:T(8,128)(2,1)} %reduce-scatter.9.cloned.1.call-done), channel_id=1, source_target_pairs={{0,0},{1,4},{2,8},{3,12},{4,1},{5,5},{6,9},{7,13},{8,2},{9,6},{10,... | collective-permute-start | bytes 294920 | tf_op jit(solution)/shard_map/ppermute | solution.py:56
  239.0 167.9 %reduce-scatter.7.cloned.1.call-start = ((), (), s32[]{:S(2)}) async-start(), calls=%async_computation.6 | async-start | bytes 8355840 | tf_op jit(solution)/shard_map/reduce_scatter | solution.py:72
  239.0 1.2 collective-permute-start.1
  272.5 1.7 collective-permute-start.3
Sparse Core Ops, SparseCore 0:
  12.1 119.9 all-gather.4
  134.2 35.0 all-gather.2
  171.8 20.2 reduce-scatter.8
  194.8 21.1 reduce-scatter.4
  239.1 33.3 reduce-scatter.10
  275.3 131.5 reduce-scatter.6

commit v2 on v1

--- a/solution.py
+++ b/solution.py
@@ -1,9 +1,14 @@
+import functools
+
 import jax
 import jax.numpy as jnp
 from jax import lax
+from jax.experimental import pallas as pl
+from jax.experimental.pallas import tpu as pltpu
 from jax.sharding import PartitionSpec as P
 
 HD = 192
+MESH = pl.DeviceIdType.MESH
 
 
 def contract_last(left, right):
@@ -45,6 +50,176 @@
     return (queries, grad_tokens)
 
 
+def exchange_kernel(
+    n, chunks, tile, latent_ref, w_ref, keep_ref, cot_ref, queries_ref, grad_ref,
+    masked_w, parts, landed, total, send_sem, recv_sem,
+):
+    me = lax.axis_index("dp")
+    count, cols = cot_ref.shape
+    rows = count // chunks
+
+    barrier = pltpu.get_barrier_semaphore()
+    for step in (1, n - 1):
+        pl.semaphore_signal(
+            barrier, inc=1, device_id={"dp": lax.rem(me + step, n)}, device_id_type=MESH
+        )
+    pl.semaphore_wait(barrier, 2)
+
+    ways = (
+        (me, lax.rem(me + 1, n), me < n - 1, me > 0),
+        (n - 1 - me, lax.rem(me + n - 1, n), me > 0, me < n - 1),
+    )
+
+    def span(k):
+        return pl.ds(pl.multiple_of(k * rows, rows), rows)
+
+    def copy(way, source, round_, k):
+        return pltpu.make_async_remote_copy(
+            src_ref=source,
+            dst_ref=landed.at[way, round_, span(k)],
+            send_sem=send_sem.at[way, round_, k],
+            recv_sem=recv_sem.at[way, round_, k],
+            device_id={"dp": ways[way][1]},
+            device_id_type=MESH,
+        )
+
+    def start_own(way):
+        @pl.when(ways[way][2])
+        def _():
+            @pl.loop(0, chunks)
+            def _(k):
+                copy(way, cot_ref.at[span(k)], 0, k).start()
+
+    def column_tiles(body):
+        @pl.loop(0, cols // tile)
+        def _(c):
+            body(pl.ds(pl.multiple_of(c * tile, tile), tile))
+
+    def grad_of(read, block):
+        total[...] = jnp.zeros_like(total)
+
+        def add(at):
+            total[...] += contract_last(read(at), masked_w[:, at])
+
+        column_tiles(add)
+        grad_ref[block] = total[...].astype(grad_ref.dtype)
+
+    start_own(0)
+    start_own(1)
+
+    def query_tile(at):
+        w = w_ref[:, at] * keep_ref[:, at]
+        masked_w[:, at] = w
+        product = jnp.dot(latent_ref[...], w, preferred_element_type=jnp.float32)
+        parts[:, :, at] = product.astype(parts.dtype).reshape(n, count, tile)
+
+    column_tiles(query_tile)
+    grad_of(lambda at: cot_ref[:, at], me)
+
+    for round_ in range(1, n):
+
+        @pl.loop(0, chunks)
+        def _(k):
+            for way in (0, 1):
+                place, _, has_next, has_prev = ways[way]
+                at = span(k)
+
+                @pl.when(has_prev)
+                def _():
+                    copy(way, landed.at[way, round_ - 1, at], round_ - 1, k).wait_recv()
+
+                @pl.when(jnp.logical_and(has_next, place >= round_))
+                def _():
+                    copy(way, landed.at[way, round_ - 1, at], round_, k).start()
+
+                @pl.when(jnp.logical_and(has_next, place < round_))
+                def _():
+                    ahead = place + n - round_
+                    owner = ahead if way == 0 else n - 1 - ahead
+
+                    @pl.when(has_prev)
+                    def _():
+                        def add(cs):
+                            both = parts[owner, at, cs].astype(jnp.float32) + landed[
+                                way, round_ - 1, at, cs
+                            ].astype(jnp.float32)
+                            parts[owner, at, cs] = both.astype(parts.dtype)
+
+                        column_tiles(add)
+
+                    copy(way, parts.at[owner, at], round_, k).start()
+
+        for way in (0, 1):
+            place = ways[way][0]
+
+            @pl.when(place >= round_)
+            def _():
+                block = me - round_ if way == 0 else me + round_
+                grad_of(lambda at: landed[way, round_ - 1, :, at], block)
+
+    @pl.loop(0, chunks)
+    def _(k):
+        at = span(k)
+        for way in (0, 1):
+
+            @pl.when(ways[way][3])
+            def _():
+                copy(way, landed.at[way, n - 1, at], n - 1, k).wait_recv()
+
+        def finish(used):
+            def add(cs):
+                value = parts[me, at, cs].astype(jnp.float32)
+                for way in used:
+                    value += landed[way, n - 1, at, cs].astype(jnp.float32)
+                queries_ref[at, cs] = value.astype(queries_ref.dtype)
+
+            column_tiles(add)
+
+        pl.when(me == 0)(lambda: finish((1,)))
+        pl.when(me == n - 1)(lambda: finish((0,)))
+        pl.when(jnp.logical_and(me > 0, me < n - 1))(lambda: finish((0, 1)))
+
+    for way in (0, 1):
+
+        @pl.when(ways[way][2])
+        def _():
+            for round_ in range(n):
+
+                @pl.loop(0, chunks)
+                def _(k):
+                    copy(way, landed.at[way, round_, span(k)], round_, k).wait_send()
+
+
+def exchange(latent, w_up, keep, cotangent):
+    n = lax.axis_size("dp")
+    count, cols = cotangent.shape
+    depth = w_up.shape[0]
+    chunks = 4
+    tile = 384 if cols % 384 == 0 else 128
+    vmem = pl.BlockSpec(memory_space=pltpu.VMEM)
+    bf16 = jnp.bfloat16
+    return pl.pallas_call(
+        functools.partial(exchange_kernel, n, chunks, tile),
+        out_shape=(
+            jax.ShapeDtypeStruct((count, cols), bf16),
+            jax.ShapeDtypeStruct((n, count, depth), bf16),
+        ),
+        in_specs=[vmem] * 4,
+        out_specs=(vmem, vmem),
+        scratch_shapes=[
+            pltpu.VMEM((depth, cols), bf16),
+            pltpu.VMEM((n, count, cols), bf16),
+            pltpu.VMEM((2, n, count, cols), bf16),
+            pltpu.VMEM((count, depth), jnp.float32),
+            pltpu.SemaphoreType.DMA((2, n, chunks)),
+            pltpu.SemaphoreType.DMA((2, n, chunks)),
+        ],
+        compiler_params=pltpu.CompilerParams(
+            collective_id=0, has_side_effects=True, vmem_limit_bytes=60 * 2**20
+        ),
+    )(latent, w_up, keep, cotangent)
+
+
 def move_tokens_body(tokens, w_down, gain, w_up, head_counts, cotangent):
     n = lax.axis_size("mp")
     swap = [(i * n + j, j * n + i) for i in range(n) for j in range(n)]
@@ -64,13 +239,9 @@
     root_mean = jnp.sqrt(squares / latent_width + 1e-06)
     latent_local = (latent_raw / root_mean * gain).astype(jnp.bfloat16)
     latent = lax.all_gather(transpose_owner(latent_local), "mp", axis=0, tiled=True)
-    query_partial = (
-        jnp.dot(latent, w_up, preferred_element_type=jnp.float32) * keep_mask
-    ).astype(jnp.bfloat16)
-    masked = cotangent * keep_mask.astype(jnp.bfloat16)
-    masked_all = lax.all_gather(masked, "dp", axis=0, tiled=True)
-    queries = lax.psum_scatter(query_partial, "dp", scatter_dimension=0, tiled=True)
-    grad_partial = contract_last(masked_all, w_up).astype(jnp.bfloat16)
+    keep_row = keep_mask.astype(jnp.bfloat16)[None, :]
+    queries, grad_partial = exchange(latent, w_up, keep_row, cotangent)
+    grad_partial = grad_partial.reshape(-1, grad_partial.shape[-1])
     grad_latent = transpose_owner(
         lax.psum_scatter(grad_partial, "mp", scatter_dimension=0, tiled=True)
     ).astype(jnp.float32)

time: 415 us -> 380 us (0.916)
  the two profiles are of different devices: /device:TPU:9 before, /device:TPU:2 now
where the time goes in v2:
time: 380 us; the launch traced here: 379 us
  Pallas kernels  152 us (40%)
  waiting for transfers between devices  146 us (38%)
  blocking collectives  33.1 us (9%)
  starting transfers between devices  18.5 us (5%)
  between operations  13.9 us (4%)
  matrix products  7.75 us (2%)
  local copies, waits for them, and re-layouts  4.83 us (1%)
    pallas_call x1, Pallas kernels, exchange(): pl.pallas_call(functools.partial(exchange_kernel, n, chunks, tile), out_s...  152 us
    ppermute x4, waiting for transfers between devices, transpose_owner(): return lax.ppermute(block, ('dp', 'mp'), swap)  54.3 us
    reduce_scatter x1, waiting for transfers between devices, move_tokens_body(): lax.psum_scatter(token_partial, 'mp', scatter_dimension=0, tiled=True)  29.4 us
    reduce_scatter x1, waiting for transfers between devices, move_tokens_body(): lax.psum_scatter(raw_partial, 'dp', scatter_dimension=0, tiled=True)  23.8 us
    reduce_scatter x1, waiting for transfers between devices, move_tokens_body(): lax.psum_scatter(grad_partial, 'mp', scatter_dimension=0, tiled=True)  19.9 us
    all_gather x1, waiting for transfers between devices, move_tokens_body(): lax.all_gather(transpose_owner(tokens_block), 'mp', axis=0, tiled=True)  18.7 us
    ppermute x4, starting transfers between devices, transpose_owner(): return lax.ppermute(block, ('dp', 'mp'), swap)  18.4 us
    all_gather x1, blocking collectives, move_tokens_body(): grad_raw_all = lax.all_gather(grad_raw, 'dp', axis=0, tiled=True)  14.8 us
  transfers between devices with their start and end apart: 8, of which 8 were waited for; matrix products, arithmetic and copies ran while one was open for 0% of the time, Pallas kernels for 0%

profile of v2, /device:TPU:2, one launch (start us, length us, event | category | flops | bytes accessed | tf_op | source)
XLA Modules:
  0.0 379.4 jit_solution(17431155866115332925)
XLA Ops:
  7.2 0.0 copy-start
  7.2 0.0 all-gather.2.cloned.1.call-start
  7.2 1.4 copy-done
  8.7 4.5 %collective-permute-start = (bf16[128,1792]{1,0:T(8,128)(2,1)S(1)}, bf16[128,1792]{1,0:T(8,128)(2,1)S(1)}, u32[]{:S(2)}, u32[]{:S(2)}) collective-permute-start(bf16[128,1792]{1,0:T(8,128)(2,1)S(1)} %constant_dynamic-slice_fusion), channel_id=1, source_target_pairs={{0,0},{1,4},{2,8},{3,12},{4,1},{5,5},{6,9},{7,13},{8,2},{9,6},{10,... | collective-permute-start | bytes 1376264 | tf_op jit(solution)/shard_map/ppermute | solution.py:231
  13.2 22.0 %collective-permute-done = bf16[128,1792]{1,0:T(8,128)(2,1)S(1)} collective-permute-done((bf16[128,1792]{1,0:T(8,128)(2,1)S(1)}, bf16[128,1792]{1,0:T(8,128)(2,1)S(1)}, u32[]{:S(2)}, u32[]{:S(2)}) %collective-permute-start) | collective-permute-done | bytes 458784 | tf_op jit(solution)/shard_map/ppermute | solution.py:231
  35.2 0.0 copy-start.3
  35.2 0.8 copy-done.3
  35.9 0.0 all-gather.2.cloned.1.call-update
  36.0 0.0 copy-start.5
  36.0 0.0 copy-start.4
  36.0 0.0 reduce-scatter.4.cloned.1.call-start
  36.0 18.7 %all-gather.2.cloned.1.call-done = bf16[512,1792]{1,0:T(8,128)(2,1)} async-done(((bf16[128,1792]{1,0:T(8,128)(2,1)}), bf16[512,1792]{1,0:T(8,128)(2,1)}) %all-gather.2.cloned.1.call-update) | async-done | bytes 1835024 | tf_op jit(solution)/shard_map/all_gather | solution.py:235
  54.7 3.9 %fusion.4 = f32[512,384]{1,0:T(8,128)} fusion(bf16[512,1792]{1,0:T(8,128)(2,1)} %all-gather.2.cloned.1.call-done, bf16[1792,384]{1,0:T(8,128)(2,1)} %param.7), kind=kOutput, calls=%fused_computation.18 | convolution fusion | flops 704643072 | bytes 3997696 | tf_op jit(solution)/shard_map/dot_general | solution.py:236
  58.6 0.0 reduce-scatter.4.cloned.1.call-update
  58.6 0.0 reduce-scatter.6.cloned.1.call-start
  58.7 0.0 copy-done.5
  58.7 0.6 dynamic_slice.7
  59.3 23.8 %reduce-scatter.4.cloned.1.call-done = f32[128,384]{1,0:T(8,128)} async-done(((f32[512,384]{1,0:T(8,128)}), f32[128,384]{1,0:T(8,128)}) %reduce-scatter.4.cloned.1.call-update) | async-done | bytes 196624 | tf_op jit(solution)/shard_map/reduce_scatter | solution.py:237
  83.1 1.0 multiply_reduce_fusion.1
  84.1 5.9 %psum.14 = f32[128,1]{0,1:T(1,128)S(1)} all-reduce(f32[128,1]{0,1:T(1,128)S(1)} %bitcast.12), channel_id=1, replica_groups=mesh['groups'=2,'dp'=4,'mp'=4] {'mp'}, use_global_device_ids=true, to_apply=%region_2.3 | all-reduce | flops 128 | bytes 1024 | tf_op jit(solution)/shard_map/psum | solution.py:238
  90.1 0.0 copy-done.4
  90.1 1.0 multiply_convert_fusion
  91.1 3.1 collective-permute-start.1
  94.2 1.3 fusion.keep_ref
  95.4 5.1 %collective-permute-done.1 = bf16[128,384]{1,0:T(8,128)(2,1)S(1)} collective-permute-done((bf16[128,384]{1,0:T(8,128)(2,1)S(1)}, bf16[128,384]{1,0:T(8,128)(2,1)S(1)}, u32[]{:S(2)}, u32[]{:S(2)}) %collective-permute-start.1) | collective-permute-done | bytes 98336 | tf_op jit(solution)/shard_map/ppermute | solution.py:231
  100.5 6.6 %all_gather.10.latent_ref = bf16[512,384]{1,0:T(8,128)(2,1)} all-gather(bf16[128,384]{1,0:T(8,128)(2,1)S(1)} %collective-permute-done.1), channel_id=1, replica_groups=mesh['groups'=2,'dp'=4,'mp'=4] {'mp'}, dimensions={0}, use_global_device_ids=true | all-gather | bytes 491520 | tf_op jit(solution)/shard_map/all_gather | solution.py:241
  107.1 0.0 copy-start.1
  107.1 151.5 %shard_map.77 = (bf16[128,6528]{1,0:T(8,128)(2,1)}, bf16[4,128,384]{2,1,0:T(8,128)(2,1)}) custom-call(bf16[512,384]{1,0:T(8,128)(2,1)} %all_gather.10.latent_ref, bf16[384,6528]{1,0:T(8,128)(2,1)} %w_ref.1, bf16[1,6528]{1,0:T(2,128)(2,1)} %fusion.keep_ref, bf16[128,6528]{1,0:T(8,128)(2,1)} %cot_ref.1), custom_call_target="tpu_custom_call" | custom-call | tf_op jit(solution)/shard_map/pallas_call | solution.py:201
  258.7 0.0 reduce-scatter.6.cloned.1.call-update
  258.7 0.0 reduce-scatter.8.cloned.1.call-start
  258.7 19.9 %reduce-scatter.6.cloned.1.call-done = bf16[128,384]{1,0:T(8,128)(2,1)} async-done(((bf16[512,384]{1,0:T(8,128)(2,1)}), bf16[128,384]{1,0:T(8,128)(2,1)}) %reduce-scatter.6.cloned.1.call-update) | async-done | bytes 98320 | tf_op jit(solution)/shard_map/reduce_scatter | solution.py:246
  278.6 5.4 %collective-permute-start.2 = (bf16[128,384]{1,0:T(8,128)(2,1)}, bf16[128,384]{1,0:T(8,128)(2,1)S(1)}, u32[]{:S(2)}, u32[]{:S(2)}) collective-permute-start(bf16[128,384]{1,0:T(8,128)(2,1)} %reduce-scatter.6.cloned.1.call-done), channel_id=1, source_target_pairs={{0,0},{1,4},{2,8},{3,12},{4,1},{5,5},{6,9},{7,13},{8,2},{9,6},{10,... | collective-permute-start | bytes 294920 | tf_op jit(solution)/shard_map/ppermute | solution.py:231
  284.0 5.9 %collective-permute-done.2 = bf16[128,384]{1,0:T(8,128)(2,1)S(1)} collective-permute-done((bf16[128,384]{1,0:T(8,128)(2,1)}, bf16[128,384]{1,0:T(8,128)(2,1)S(1)}, u32[]{:S(2)}, u32[]{:S(2)}) %collective-permute-start.2) | collective-permute-done | bytes 98336 | tf_op jit(solution)/shard_map/ppermute | solution.py:231
  289.9 0.0 copy-done.1
  289.9 0.1 multiply_reduce_fusion
  290.0 5.8 %psum.15 = f32[128]{0:T(128)S(1)} all-reduce(f32[128]{0:T(128)S(1)} %multiply_reduce_fusion), channel_id=1, replica_groups=mesh['groups'=2,'dp'=4,'mp'=4] {'mp'}, use_global_device_ids=true, to_apply=%region_5.6 | all-reduce | flops 128 | bytes 1024 | tf_op jit(solution)/shard_map/psum | solution.py:248
  295.8 0.1 subtract_convert_fusion
  295.9 14.8 %all_gather.11 = bf16[512,384]{1,0:T(8,128)(2,1)S(1)} all-gather(bf16[128,384]{1,0:T(8,128)(2,1)S(1)} %subtract_convert_fusion), channel_id=1, replica_groups=mesh['groups'=2,'dp'=4,'mp'=4] {'dp'}, dimensions={0}, use_global_device_ids=true | all-gather | bytes 491520 | tf_op jit(solution)/shard_map/all_gather | solution.py:252
  310.8 0.0 copy-start.2
  310.8 3.9 %convolution_convert_fusion = bf16[512,1792]{1,0:T(8,128)(2,1)} fusion(bf16[512,384]{1,0:T(8,128)(2,1)S(1)} %all_gather.11, bf16[1792,384]{1,0:T(8,128)(2,1)} %param.7), kind=kOutput, calls=%fused_computation | convolution fusion | flops 705560576 | bytes 3604480 | tf_op jit(solution)/shard_map/dot_general | solution.py:15
  314.7 0.0 reduce-scatter.8.cloned.1.call-update
  314.7 29.4 %reduce-scatter.8.cloned.1.call-done = bf16[128,1792]{1,0:T(8,128)(2,1)} async-done(((bf16[512,1792]{1,0:T(8,128)(2,1)}), bf16[128,1792]{1,0:T(8,128)(2,1)}) %reduce-scatter.8.cloned.1.call-update) | async-done | bytes 458768 | tf_op jit(solution)/shard_map/reduce_scatter | solution.py:255
  344.1 5.4 %collective-permute-start.3 = (bf16[128,1792]{1,0:T(8,128)(2,1)}, bf16[128,1792]{1,0:T(8,128)(2,1)S(1)}, u32[]{:S(2)}, u32[]{:S(2)}) collective-permute-start(bf16[128,1792]{1,0:T(8,128)(2,1)} %reduce-scatter.8.cloned.1.call-done), channel_id=1, source_target_pairs={{0,0},{1,4},{2,8},{3,12},{4,1},{5,5},{6,9},{7,13},{8,2},{9,6},{10,... | collective-permute-start | bytes 1376264 | tf_op jit(solution)/shard_map/ppermute | solution.py:231
  349.6 21.3 %collective-permute-done.3 = bf16[128,1792]{1,0:T(8,128)(2,1)S(1)} collective-permute-done((bf16[128,1792]{1,0:T(8,128)(2,1)}, bf16[128,1792]{1,0:T(8,128)(2,1)S(1)}, u32[]{:S(2)}, u32[]{:S(2)}) %collective-permute-start.3) | collective-permute-done | bytes 458784 | tf_op jit(solution)/shard_map/ppermute | solution.py:231
  370.9 0.0 copy-done.2
  370.9 1.2 copy.10
  372.1 0.8 copy.11
  (2 shorter events, 0.0 us)
Async XLA Ops:
  7.2 1.5 copy-start
  7.2 47.6 %all-gather.2.cloned.1.call-start = ((), (), s32[]{:S(2)}) async-start(), calls=%async_computation.3 | async-start | bytes 2293760 | tf_op jit(solution)/shard_map/all_gather | solution.py:235
  8.7 26.5 %collective-permute-start = (bf16[128,1792]{1,0:T(8,128)(2,1)S(1)}, bf16[128,1792]{1,0:T(8,128)(2,1)S(1)}, u32[]{:S(2)}, u32[]{:S(2)}) collective-permute-start(bf16[128,1792]{1,0:T(8,128)(2,1)S(1)} %constant_dynamic-slice_fusion), channel_id=1, source_target_pairs={{0,0},{1,4},{2,8},{3,12},{4,1},{5,5},{6,9},{7,13},{8,2},{9,6},{10,... | collective-permute-start | bytes 1376264 | tf_op jit(solution)/shard_map/ppermute | solution.py:231
  35.2 0.8 copy-start.3
  36.0 22.7 %copy-start.5 = (s32[4]{0:T(128)S(1)}, s32[4]{0:T(128)}, u32[]{:S(2)}) copy-start(s32[4]{0:T(128)} %param.10) | copy-start | bytes 52
  36.0 54.1 %copy-start.4 = (f32[384]{0:T(512)S(1)}, f32[384]{0:T(512)}, u32[]{:S(2)}) copy-start(f32[384]{0:T(512)} %param.8) | copy-start | bytes 4612
  36.0 47.1 %reduce-scatter.4.cloned.1.call-start = ((), (), s32[]{:S(2)}) async-start(), calls=%async_computation.4 | async-start | bytes 983040 | tf_op jit(solution)/shard_map/reduce_scatter | solution.py:237
  58.6 219.9 %reduce-scatter.6.cloned.1.call-start = ((), (), s32[]{:S(2)}) async-start(), calls=%async_computation.5 | async-start | bytes 491520 | tf_op jit(solution)/shard_map/reduce_scatter | solution.py:246
  91.1 9.4 %collective-permute-start.1 = (bf16[128,384]{1,0:T(8,128)(2,1)S(1)}, bf16[128,384]{1,0:T(8,128)(2,1)S(1)}, u32[]{:S(2)}, u32[]{:S(2)}) collective-permute-start(bf16[128,384]{1,0:T(8,128)(2,1)S(1)} %multiply_convert_fusion), channel_id=1, source_target_pairs={{0,0},{1,4},{2,8},{3,12},{4,1},{5,5},{6,9},{7,13},{8,2},{9,6},{10,... | collective-permute-start | bytes 294920 | tf_op jit(solution)/shard_map/ppermute | solution.py:231
  107.1 182.8 %copy-start.1 = (f32[128,384]{1,0:T(8,128)S(1)}, f32[128,384]{1,0:T(8,128)}, u32[]{:S(2)}) copy-start(f32[128,384]{1,0:T(8,128)} %reduce-scatter.4.cloned.1.call-done) | copy-start | bytes 589828
  258.7 85.4 %reduce-scatter.8.cloned.1.call-start = ((), (), s32[]{:S(2)}) async-start(), calls=%async_computation.6 | async-start | bytes 2293760 | tf_op jit(solution)/shard_map/reduce_scatter | solution.py:255
  278.6 11.3 %collective-permute-start.2 = (bf16[128,384]{1,0:T(8,128)(2,1)}, bf16[128,384]{1,0:T(8,128)(2,1)S(1)}, u32[]{:S(2)}, u32[]{:S(2)}) collective-permute-start(bf16[128,384]{1,0:T(8,128)(2,1)} %reduce-scatter.6.cloned.1.call-done), channel_id=1, source_target_pairs={{0,0},{1,4},{2,8},{3,12},{4,1},{5,5},{6,9},{7,13},{8,2},{9,6},{10,... | collective-permute-start | bytes 294920 | tf_op jit(solution)/shard_map/ppermute | solution.py:231
  310.8 60.1 %copy-start.2 = (bf16[128,6528]{1,0:T(8,128)(2,1)S(1)}, bf16[128,6528]{1,0:T(8,128)(2,1)}, u32[]{:S(2)}) copy-start(bf16[128,6528]{1,0:T(8,128)(2,1)} %get-tuple-element.10) | copy-start | bytes 5013508
  344.1 26.8 %collective-permute-start.3 = (bf16[128,1792]{1,0:T(8,128)(2,1)}, bf16[128,1792]{1,0:T(8,128)(2,1)S(1)}, u32[]{:S(2)}, u32[]{:S(2)}) collective-permute-start(bf16[128,1792]{1,0:T(8,128)(2,1)} %reduce-scatter.8.cloned.1.call-done), channel_id=1, source_target_pairs={{0,0},{1,4},{2,8},{3,12},{4,1},{5,5},{6,9},{7,13},{8,2},{9,6},{10,... | collective-permute-start | bytes 1376264 | tf_op jit(solution)/shard_map/ppermute | solution.py:231
Sparse Core Ops, SparseCore 0:
  36.1 18.6 all-gather.1
  58.8 24.2 reduce-scatter.3
  258.8 19.7 reduce-scatter.5
  314.8 29.2 reduce-scatter.7

commit v3 on v2

--- a/solution.py
+++ b/solution.py
@@ -51,19 +51,37 @@
 
 
 def exchange_kernel(
-    n, chunks, tile, latent_ref, w_ref, keep_ref, cot_ref, queries_ref, grad_ref,
+    n, chunks, tile, tokens_ref, down_ref, gain_ref, w_ref, keep_ref, cot_ref,
+    queries_ref, grad_ref, raw_ref, root_ref,
     masked_w, parts, landed, total, send_sem, recv_sem,
+    tokens_all, raw_total, raw_out, raw_in, square_out, square_in, latent_out, latent_all,
+    small_send, small_recv,
 ):
     me = lax.axis_index("dp")
     count, cols = cot_ref.shape
     rows = count // chunks
 
+    mine = lax.axis_index("mp")
+
     barrier = pltpu.get_barrier_semaphore()
-    for step in (1, n - 1):
-        pl.semaphore_signal(
-            barrier, inc=1, device_id={"dp": lax.rem(me + step, n)}, device_id_type=MESH
+
+    @pl.loop(0, n * n)
+    def _(other):
+        @pl.when(other != me * n + mine)
+        def _():
+            pl.semaphore_signal(
+                barrier, inc=1,
+                device_id={"dp": other // n, "mp": lax.rem(other, n)}, device_id_type=MESH,
+            )
+
+    pl.semaphore_wait(barrier, n * n - 1)
+
+    def small(kind, slot, source, target, dp, mp):
+        return pltpu.make_async_remote_copy(
+            src_ref=source, dst_ref=target,
+            send_sem=small_send.at[kind, slot], recv_sem=small_recv.at[kind, slot],
+            device_id={"dp": dp, "mp": mp}, device_id_type=MESH,
         )
-    pl.semaphore_wait(barrier, 2)
 
     ways = (
         (me, lax.rem(me + 1, n), me < n - 1, me > 0),
@@ -83,10 +101,10 @@
             device_id_type=MESH,
         )
 
-    def start_own(way):
+    def start_own(way, first, last):
         @pl.when(ways[way][2])
         def _():
-            @pl.loop(0, chunks)
+            @pl.loop(first, last)
             def _(k):
                 copy(way, cot_ref.at[span(k)], 0, k).start()
 
@@ -104,13 +122,117 @@
         column_tiles(add)
         grad_ref[block] = total[...].astype(grad_ref.dtype)
 
-    start_own(0)
-    start_own(1)
+    down_rows, width = down_ref.shape
+    quarter = count // n
+    far, near = lax.rem(mine + 2, n), mine + 1 - 2 * lax.rem(mine, 2)
+    far_near = lax.rem(near + 2, n)
+
+    def after(o):
+        return lax.rem(me + o, n)
+
+    def before(o):
+        return lax.rem(me + n - o, n)
+
+    def piece(block, who):
+        return tokens_all.at[block, pl.ds(pl.multiple_of(who * quarter, quarter), quarter)]
+
+    def token_columns(block):
+        return pl.ds(pl.multiple_of(block * down_rows, down_rows), down_rows)
+
+    started = []
+
+    def go(c):
+        c.start()
+        started.append(c)
+
+    for o in range(1, n):
+        source = tokens_ref.at[
+            pl.ds(pl.multiple_of(mine * quarter, quarter), quarter), token_columns(after(o))
+        ]
+        go(small(0, o, source, piece(me, mine), after(o), mine))
+    for way in (0, 1):
+        start_own(way, 0, chunks // 2)
+    tokens_all[me] = tokens_ref[:, token_columns(me)]
+    for o in range(1, n):
+        block = before(o)
+        held = piece(block, mine)
+        small(0, o, held, held, me, far).wait_recv()
+        go(small(1, o, held, held, me, far))
+        go(small(2, o, held, held, me, near))
+    for o in range(1, n):
+        held = piece(before(o), far)
+        small(1, o, held, held, me, far).wait_recv()
+        go(small(3, o, held, held, me, near))
+    for o in range(1, n):
+        for kind, who in ((2, near), (3, far_near)):
+            held = piece(before(o), who)
+            small(kind, o, held, held, me, near).wait_recv()
+
+    raw_total[...] = jnp.zeros_like(raw_total)
+    depth_tile = 256 if down_rows % 256 == 0 else 128
+
+    @pl.loop(0, down_rows // depth_tile)
+    def _(c):
+        at = pl.ds(pl.multiple_of(c * depth_tile, depth_tile), depth_tile)
+        raw_total[...] += jnp.dot(
+            tokens_all[:, :, at].reshape(n * count, depth_tile), down_ref[at, :],
+            preferred_element_type=jnp.float32,
+        )
+
+    raw_out[...] = raw_total[...].astype(raw_out.dtype).reshape(raw_out.shape)
+    for o in range(1, n):
+        go(small(4, o, raw_out.at[after(o)], raw_in.at[o - 1], after(o), mine))
+    for way in (0, 1):
+        start_own(way, chunks // 2, chunks)
+    raw = raw_total[pl.ds(pl.multiple_of(me * count, count), count), :]
+    for o in range(1, n):
+        small(4, o, raw_out.at[me], raw_in.at[o - 1], after(o), mine).wait_recv()
+        raw += raw_in[o - 1].astype(jnp.float32)
+    raw_ref[...] = raw
+    square_out[...] = jnp.broadcast_to(
+        jnp.sum(raw * raw, axis=1, keepdims=True), square_out.shape
+    )
+    for o in range(1, n):
+        go(small(5, o, square_out, square_in.at[o - 1], me, lax.rem(mine + o, n)))
+    squares = square_out[...]
+    for o in range(1, n):
+        small(5, o, square_out, square_in.at[o - 1], me, mine).wait_recv()
+        squares += square_in[o - 1]
+    root = jnp.sqrt(squares / (width * n) + 1e-06)
+    root_ref[...] = root
+    latent_out[...] = (raw_ref[...] / root[:, :1] * gain_ref[...]).astype(latent_out.dtype)
+
+    on_diagonal = me == mine
+
+    def latent_slot(block):
+        return latent_all.at[pl.ds(pl.multiple_of(block * count, count), count)]
+
+    def latent_copy(to):
+        return pltpu.make_async_remote_copy(
+            src_ref=latent_out, dst_ref=latent_slot(me),
+            send_sem=small_send.at[6, to], recv_sem=small_recv.at[6, me],
+            device_id={"dp": mine, "mp": to}, device_id_type=MESH,
+        )
+
+    for to in range(n):
+        itself = jnp.logical_and(on_diagonal, mine == to)
+        pl.when(jnp.logical_not(itself))(lambda to=to: latent_copy(to).start())
+
+    @pl.when(on_diagonal)
+    def _():
+        latent_all[pl.ds(pl.multiple_of(me * count, count), count), :] = latent_out[...]
+
+    for block in range(n):
+        itself = jnp.logical_and(on_diagonal, me == block)
+
+        @pl.when(jnp.logical_not(itself))
+        def _():
+            small(6, block, latent_out, latent_slot(block), me, near).wait_recv()
 
     def query_tile(at):
         w = w_ref[:, at] * keep_ref[:, at]
         masked_w[:, at] = w
-        product = jnp.dot(latent_ref[...], w, preferred_element_type=jnp.float32)
+        product = jnp.dot(latent_all[...], w, preferred_element_type=jnp.float32)
         parts[:, :, at] = product.astype(parts.dtype).reshape(n, count, tile)
 
     column_tiles(query_tile)
@@ -189,8 +311,14 @@
                 def _(k):
                     copy(way, landed.at[way, round_, span(k)], round_, k).wait_send()
 
-
-def exchange(latent, w_up, keep, cotangent):
+    for c in started:
+        c.wait_send()
+    for to in range(n):
+        itself = jnp.logical_and(on_diagonal, mine == to)
+        pl.when(jnp.logical_not(itself))(lambda to=to: latent_copy(to).wait_send())
+
+
+def exchange(tokens, w_down, gain, w_up, keep, cotangent):
     n = lax.axis_size("dp")
     count, cols = cotangent.shape
     depth = w_up.shape[0]
@@ -203,9 +331,11 @@
         out_shape=(
             jax.ShapeDtypeStruct((count, cols), bf16),
             jax.ShapeDtypeStruct((n, count, depth), bf16),
+            jax.ShapeDtypeStruct((count, depth), jnp.float32),
+            jax.ShapeDtypeStruct((count, 128), jnp.float32),
         ),
-        in_specs=[vmem] * 4,
-        out_specs=(vmem, vmem),
+        in_specs=[vmem] * 6,
+        out_specs=(vmem,) * 4,
         scratch_shapes=[
             pltpu.VMEM((depth, cols), bf16),
             pltpu.VMEM((n, count, cols), bf16),
@@ -213,34 +343,37 @@
             pltpu.VMEM((count, depth), jnp.float32),
             pltpu.SemaphoreType.DMA((2, n, chunks)),
             pltpu.SemaphoreType.DMA((2, n, chunks)),
+            pltpu.VMEM((n, count, w_down.shape[0]), bf16),
+            pltpu.VMEM((n * count, depth), jnp.float32),
+            pltpu.VMEM((n, count, depth), bf16),
+            pltpu.VMEM((n - 1, count, depth), bf16),
+            pltpu.VMEM((count, 128), jnp.float32),
+            pltpu.VMEM((n - 1, count, 128), jnp.float32),
+            pltpu.VMEM((count, depth), bf16),
+            pltpu.VMEM((n * count, depth), bf16),
+            pltpu.SemaphoreType.DMA((7, n)),
+            pltpu.SemaphoreType.DMA((7, n)),
         ],
         compiler_params=pltpu.CompilerParams(
             collective_id=0, has_side_effects=True, vmem_limit_bytes=60 * 2**20
         ),
-    )(latent, w_up, keep, cotangent)
+    )(tokens, w_down, gain, w_up, keep, cotangent)
 
 
 def move_tokens_body(tokens, w_down, gain, w_up, head_counts, cotangent):
     n = lax.axis_size("mp")
     swap = [(i * n + j, j * n + i) for i in range(n) for j in range(n)]
-    position = lax.axis_index("mp")
     latent_width = w_down.shape[1] * n
     keep_mask = keep_mask_of(head_counts, w_up.shape[1])
 
     def transpose_owner(block):
         return lax.ppermute(block, ("dp", "mp"), swap)
 
-    rows = w_down.shape[0]
-    tokens_block = lax.dynamic_slice_in_dim(tokens, position * rows, rows, 1)
-    tokens_cols = lax.all_gather(transpose_owner(tokens_block), "mp", axis=0, tiled=True)
-    raw_partial = jnp.dot(tokens_cols, w_down, preferred_element_type=jnp.float32)
-    latent_raw = lax.psum_scatter(raw_partial, "dp", scatter_dimension=0, tiled=True)
-    squares = lax.psum(jnp.sum(latent_raw * latent_raw, axis=1, keepdims=True), "mp")
-    root_mean = jnp.sqrt(squares / latent_width + 1e-06)
-    latent_local = (latent_raw / root_mean * gain).astype(jnp.bfloat16)
-    latent = lax.all_gather(transpose_owner(latent_local), "mp", axis=0, tiled=True)
     keep_row = keep_mask.astype(jnp.bfloat16)[None, :]
-    queries, grad_partial = exchange(latent, w_up, keep_row, cotangent)
+    queries, grad_partial, latent_raw, root_mean = exchange(
+        tokens, w_down, gain[None, :], w_up, keep_row, cotangent
+    )
+    root_mean = root_mean[:, :1]
     grad_partial = grad_partial.reshape(-1, grad_partial.shape[-1])
     grad_latent = transpose_owner(
         lax.psum_scatter(grad_partial, "mp", scatter_dimension=0, tiled=True)
@@ -267,6 +400,6 @@
         P(("groups", "dp"), "mp"),
     )
     out_specs = (P(("groups", "dp"), "mp"), P(("groups", "dp"), "mp"))
-    square = mesh.shape["dp"] == mesh.shape["mp"]
+    square = mesh.shape["dp"] == mesh.shape["mp"] == 4
     body = move_tokens_body if square else gather_weights_body
     return jax.shard_map(body, mesh=mesh, in_specs=in_specs, out_specs=out_specs, check_vma=False)

time: 380 us -> 334 us (0.88)
  waiting for transfers between devices: 146 us -> 75.9 us
  Pallas kernels: 152 us -> 201 us
  blocking collectives: 33.1 us -> 20.6 us
  starting transfers between devices: 18.5 us -> 10.9 us
  matrix products: 7.75 us -> 2.41 us
    pallas_call x1, Pallas kernels: 152 us -> 201 us  [exchange(): pl.pallas_call(functools.partial(exchange_kernel, n, chunks, tile), out_s...]
    ppermute x4 -> x2, waiting for transfers between devices: 54.3 us -> 26.3 us  [transpose_owner(): return lax.ppermute(block, ('dp', 'mp'), swap)]
    reduce_scatter x1 -> x0, waiting for transfers between devices: 23.8 us -> none  [move_tokens_body(): lax.psum_scatter(raw_partial, 'dp', scatter_dimension=0, tiled=True)]
    all_gather x1 -> x0, waiting for transfers between devices: 18.7 us -> none  [move_tokens_body(): lax.all_gather(transpose_owner(tokens_block), 'mp', axis=0, tiled=True)]
    ppermute x4 -> x2, starting transfers between devices: 18.4 us -> 10.8 us  [transpose_owner(): return lax.ppermute(block, ('dp', 'mp'), swap)]
    all_gather x1 -> x0, blocking collectives: 6.57 us -> none  [move_tokens_body(): lax.all_gather(transpose_owner(latent_local), 'mp', axis=0, tiled=True)]
    psum x1 -> x0, blocking collectives: 5.9 us -> none  [move_tokens_body(): lax.psum(jnp.sum(latent_raw * latent_raw, axis=1, keepdims=True), 'mp')]
    dot_general x1 -> x0, matrix products: 3.88 us -> none  [move_tokens_body(): jnp.dot(tokens_cols, w_down, preferred_element_type=jnp.float32)]
  transfers between devices with their start and end apart: 8 -> 4, of which waited for: 8 -> 4; matrix products, arithmetic and copies ran while one was open for 0% -> 0% of each run, Pallas kernels for 0% -> 0%
where the time goes in v3:
time: 334 us; the launch traced here: 333 us
  Pallas kernels  201 us (60%)
  waiting for transfers between devices  75.9 us (23%)
  blocking collectives  20.6 us (6%)
  between operations  14.1 us (4%)
  starting transfers between devices  10.9 us (3%)
  local copies, waits for them, and re-layouts  4.44 us (1%)
  other arithmetic  4.35 us (1%)
    pallas_call x1, Pallas kernels, exchange(): pl.pallas_call(functools.partial(exchange_kernel, n, chunks, tile), out_s...  201 us
    reduce_scatter x1, waiting for transfers between devices, move_tokens_body(): lax.psum_scatter(token_partial, 'mp', scatter_dimension=0, tiled=True)  29.5 us
    ppermute x2, waiting for transfers between devices, transpose_owner(): return lax.ppermute(block, ('dp', 'mp'), swap)  26.3 us
    reduce_scatter x1, waiting for transfers between devices, move_tokens_body(): lax.psum_scatter(grad_partial, 'mp', scatter_dimension=0, tiled=True)  20.2 us
    all_gather x1, blocking collectives, move_tokens_body(): grad_raw_all = lax.all_gather(grad_raw, 'dp', axis=0, tiled=True)  14.8 us
    ppermute x2, starting transfers between devices, transpose_owner(): return lax.ppermute(block, ('dp', 'mp'), swap)  10.8 us
  transfers between devices with their start and end apart: 4, of which 4 were waited for; matrix products, arithmetic and copies ran while one was open for 0% of the time, Pallas kernels for 0%

profile of v3, /device:TPU:2, one launch (start us, length us, event | category | flops | bytes accessed | tf_op | source)
XLA Modules:
  0.0 333.5 jit_solution(9577864804652880005)
XLA Ops:
  7.2 0.0 reduce-scatter.3.cloned.1.call-start
  7.2 1.2 dynamic_slice.3
  8.5 1.3 fusion.2.keep_ref
  9.8 1.2 broadcast_in_dim.4.gain_ref
  11.0 0.0 copy-start.2
  11.0 200.7 %shard_map.77 = (bf16[128,6528]{1,0:T(8,128)(2,1)}, bf16[4,128,384]{2,1,0:T(8,128)(2,1)}, f32[128,384]{1,0:T(8,128)}, f32[128,128]{1,0:T(8,128)}) custom-call(bf16[128,7168]{1,0:T(8,128)(2,1)} %tokens_ref.1, bf16[1792,384]{1,0:T(8,128)(2,1)} %down_ref.1, f32[1,384]{1,0:T(1,128)} %broadcast_in_dim.4.gain_ref, bf16[384,6528]{1,0:T(8,128)(2,1)} %w_ref.1, ...), custom_call_target="tpu_custom_call" | custom-call | tf_op jit(solution)/shard_map/pallas_call | solution.py:329
  211.8 0.0 copy-start
  211.8 0.0 reduce-scatter.3.cloned.1.call-update
  211.8 0.0 reduce-scatter.5.cloned.1.call-start
  211.8 20.2 %reduce-scatter.3.cloned.1.call-done = bf16[128,384]{1,0:T(8,128)(2,1)} async-done(((bf16[512,384]{1,0:T(8,128)(2,1)}), bf16[128,384]{1,0:T(8,128)(2,1)}) %reduce-scatter.3.cloned.1.call-update) | async-done | bytes 98320 | tf_op jit(solution)/shard_map/reduce_scatter | solution.py:379
  232.0 5.4 %collective-permute-start = (bf16[128,384]{1,0:T(8,128)(2,1)}, bf16[128,384]{1,0:T(8,128)(2,1)S(1)}, u32[]{:S(2)}, u32[]{:S(2)}) collective-permute-start(bf16[128,384]{1,0:T(8,128)(2,1)} %reduce-scatter.3.cloned.1.call-done), channel_id=1, source_target_pairs={{0,0},{1,4},{2,8},{3,12},{4,1},{5,5},{6,9},{7,13},{8,2},{9,6},{10,... | collective-permute-start | bytes 294920 | tf_op jit(solution)/shard_map/ppermute | solution.py:370
  237.4 1.0 slice_reduce_fusion
  238.4 4.9 %collective-permute-done = bf16[128,384]{1,0:T(8,128)(2,1)S(1)} collective-permute-done((bf16[128,384]{1,0:T(8,128)(2,1)}, bf16[128,384]{1,0:T(8,128)(2,1)S(1)}, u32[]{:S(2)}, u32[]{:S(2)}) %collective-permute-start) | collective-permute-done | bytes 98336 | tf_op jit(solution)/shard_map/ppermute | solution.py:370
  243.3 0.0 copy-done.2
  243.3 1.0 multiply_reduce_fusion
  244.4 5.8 %psum.7 = f32[128]{0:T(128)S(1)} all-reduce(f32[128]{0:T(128)S(1)} %multiply_reduce_fusion), channel_id=1, replica_groups=mesh['groups'=2,'dp'=4,'mp'=4] {'mp'}, use_global_device_ids=true, to_apply=%region_2.3 | all-reduce | flops 128 | bytes 1024 | tf_op jit(solution)/shard_map/psum | solution.py:381
  250.1 1.1 subtract_convert_fusion
  251.2 14.8 %all_gather.3 = bf16[512,384]{1,0:T(8,128)(2,1)S(1)} all-gather(bf16[128,384]{1,0:T(8,128)(2,1)S(1)} %subtract_convert_fusion), channel_id=1, replica_groups=mesh['groups'=2,'dp'=4,'mp'=4] {'dp'}, dimensions={0}, use_global_device_ids=true | all-gather | bytes 491520 | tf_op jit(solution)/shard_map/all_gather | solution.py:385
  266.0 0.0 copy-done
  266.0 2.4 convolution_convert_fusion
  268.4 0.0 copy-start.1
  268.4 0.0 reduce-scatter.5.cloned.1.call-update
  268.5 29.5 %reduce-scatter.5.cloned.1.call-done = bf16[128,1792]{1,0:T(8,128)(2,1)} async-done(((bf16[512,1792]{1,0:T(8,128)(2,1)}), bf16[128,1792]{1,0:T(8,128)(2,1)}) %reduce-scatter.5.cloned.1.call-update) | async-done | bytes 458768 | tf_op jit(solution)/shard_map/reduce_scatter | solution.py:388
  297.9 5.4 %collective-permute-start.1 = (bf16[128,1792]{1,0:T(8,128)(2,1)}, bf16[128,1792]{1,0:T(8,128)(2,1)S(1)}, u32[]{:S(2)}, u32[]{:S(2)}) collective-permute-start(bf16[128,1792]{1,0:T(8,128)(2,1)} %reduce-scatter.5.cloned.1.call-done), channel_id=1, source_target_pairs={{0,0},{1,4},{2,8},{3,12},{4,1},{5,5},{6,9},{7,13},{8,2},{9,6},{10,... | collective-permute-start | bytes 1376264 | tf_op jit(solution)/shard_map/ppermute | solution.py:370
  303.3 21.3 %collective-permute-done.1 = bf16[128,1792]{1,0:T(8,128)(2,1)S(1)} collective-permute-done((bf16[128,1792]{1,0:T(8,128)(2,1)}, bf16[128,1792]{1,0:T(8,128)(2,1)S(1)}, u32[]{:S(2)}, u32[]{:S(2)}) %collective-permute-start.1) | collective-permute-done | bytes 458784 | tf_op jit(solution)/shard_map/ppermute | solution.py:370
  324.7 0.0 copy-done.1
  324.7 1.2 copy.10
  325.9 0.8 copy.11
Async XLA Ops:
  7.2 224.8 %reduce-scatter.3.cloned.1.call-start = ((), (), s32[]{:S(2)}) async-start(), calls=%async_computation.2 | async-start | bytes 491520 | tf_op jit(solution)/shard_map/reduce_scatter | solution.py:379
  11.0 232.3 %copy-start.2 = (f32[384]{0:T(512)S(1)}, f32[384]{0:T(512)}, u32[]{:S(2)}) copy-start(f32[384]{0:T(512)} %param.8) | copy-start | bytes 4612
  211.8 54.3 %copy-start = (bf16[1792,384]{1,0:T(8,128)(2,1)S(1)}, bf16[1792,384]{1,0:T(8,128)(2,1)}, u32[]{:S(2)}) copy-start(bf16[1792,384]{1,0:T(8,128)(2,1)} %down_ref.1) | copy-start | bytes 4128772
  211.8 86.1 %reduce-scatter.5.cloned.1.call-start = ((), (), s32[]{:S(2)}) async-start(), calls=%async_computation.3 | async-start | bytes 2293760 | tf_op jit(solution)/shard_map/reduce_scatter | solution.py:388
  232.0 11.3 %collective-permute-start = (bf16[128,384]{1,0:T(8,128)(2,1)}, bf16[128,384]{1,0:T(8,128)(2,1)S(1)}, u32[]{:S(2)}, u32[]{:S(2)}) collective-permute-start(bf16[128,384]{1,0:T(8,128)(2,1)} %reduce-scatter.3.cloned.1.call-done), channel_id=1, source_target_pairs={{0,0},{1,4},{2,8},{3,12},{4,1},{5,5},{6,9},{7,13},{8,2},{9,6},{10,... | collective-permute-start | bytes 294920 | tf_op jit(solution)/shard_map/ppermute | solution.py:370
  268.4 56.2 %copy-start.1 = (bf16[128,6528]{1,0:T(8,128)(2,1)S(1)}, bf16[128,6528]{1,0:T(8,128)(2,1)}, u32[]{:S(2)}) copy-start(bf16[128,6528]{1,0:T(8,128)(2,1)} %get-tuple-element.14) | copy-start | bytes 5013508
  297.9 26.8 %collective-permute-start.1 = (bf16[128,1792]{1,0:T(8,128)(2,1)}, bf16[128,1792]{1,0:T(8,128)(2,1)S(1)}, u32[]{:S(2)}, u32[]{:S(2)}) collective-permute-start(bf16[128,1792]{1,0:T(8,128)(2,1)} %reduce-scatter.5.cloned.1.call-done), channel_id=1, source_target_pairs={{0,0},{1,4},{2,8},{3,12},{4,1},{5,5},{6,9},{7,13},{8,2},{9,6},{10,... | collective-permute-start | bytes 1376264 | tf_op jit(solution)/shard_map/ppermute | solution.py:370
Sparse Core Ops, SparseCore 0:
  211.9 20.0 reduce-scatter.2
  268.6 29.2 reduce-scatter.4

commit v4 on v3

--- a/solution.py
+++ b/solution.py
@@ -52,7 +52,8 @@
 
 def exchange_kernel(
     n, chunks, tile, tokens_ref, down_ref, gain_ref, w_ref, keep_ref, cot_ref,
-    queries_ref, grad_ref, raw_ref, root_ref,
+    queries_ref, grad_tokens_ref, raw_ref, root_ref, grad_ref, grad_in, grad_all,
+    products, near_in, far_in, pair_out, block_out, block_in, dot_out, dot_in,
     masked_w, parts, landed, total, send_sem, recv_sem,
     tokens_all, raw_total, raw_out, raw_in, square_out, square_in, latent_out, latent_all,
     small_send, small_recv,
@@ -121,6 +122,22 @@
 
         column_tiles(add)
         grad_ref[block] = total[...].astype(grad_ref.dtype)
+        itself = jnp.logical_and(on_diagonal, block == me)
+
+        @pl.when(jnp.logical_not(itself))
+        def _():
+            grad_copy(block).start()
+
+        @pl.when(itself)
+        def _():
+            grad_in[mine] = grad_ref[block]
+
+    def grad_copy(block):
+        return pltpu.make_async_remote_copy(
+            src_ref=grad_ref.at[block], dst_ref=grad_in.at[mine],
+            send_sem=small_send.at[7, block], recv_sem=small_recv.at[7, mine],
+            device_id={"dp": block, "mp": me}, device_id_type=MESH,
+        )
 
     down_rows, width = down_ref.shape
     quarter = count // n
@@ -279,6 +296,33 @@
                 block = me - round_ if way == 0 else me + round_
                 grad_of(lambda at: landed[way, round_ - 1, :, at], block)
 
+    for who in range(n):
+        itself = jnp.logical_and(on_diagonal, mine == who)
+
+        @pl.when(jnp.logical_not(itself))
+        def _():
+            small(7, who, grad_ref.at[0], grad_in.at[who], me, near).wait_recv()
+
+    grad_latent = grad_in[0].astype(jnp.float32)
+    for who in range(1, n):
+        grad_latent += grad_in[who].astype(jnp.float32)
+    scaled = gain_ref[...] * grad_latent
+    raw = raw_ref[...]
+    dot_out[...] = jnp.broadcast_to(
+        jnp.sum(scaled * raw, axis=1, keepdims=True), dot_out.shape
+    )
+    for o in range(1, n):
+        go(small(8, o, dot_out, dot_in.at[o - 1], me, lax.rem(mine + o, n)))
+    inner = dot_out[...]
+    for o in range(1, n):
+        small(8, o, dot_out, dot_in.at[o - 1], me, mine).wait_recv()
+        inner += dot_in[o - 1]
+    root = root_ref[...]
+    slope = (inner / (width * n * (root * root * root)))[:, :1]
+    grad_all[me] = (scaled / root[:, :1] - raw * slope).astype(grad_all.dtype)
+    for o in range(1, n):
+        go(small(9, o, grad_all.at[me], grad_all.at[me], after(o), mine))
+
     @pl.loop(0, chunks)
     def _(k):
         at = span(k)
@@ -301,6 +345,54 @@
         pl.when(me == n - 1)(lambda: finish((0,)))
         pl.when(jnp.logical_and(me > 0, me < n - 1))(lambda: finish((0, 1)))
 
+    for o in range(1, n):
+        held = grad_all.at[before(o)]
+        small(9, o, held, held, after(o), mine).wait_recv()
+
+    def row_tiles(body):
+        @pl.loop(0, down_rows // depth_tile)
+        def _(c):
+            body(pl.ds(pl.multiple_of(c * depth_tile, depth_tile), depth_tile))
+
+    def product_tile(at):
+        product = contract_last(grad_all[...].reshape(n * count, width), down_ref[at, :])
+        products[:, :, at] = product.astype(products.dtype).reshape(n, count, depth_tile)
+
+    row_tiles(product_tile)
+    go(small(10, 0, products.at[far_near], near_in.at[1], me, near))
+    go(small(10, 1, products.at[near], near_in.at[0], me, near))
+    small(10, 0, products.at[far_near], near_in.at[1], me, near).wait_recv()
+
+    def pair_tile(at):
+        both = products[far, :, at].astype(jnp.float32) + near_in[1, :, at].astype(jnp.float32)
+        pair_out[:, at] = both.astype(pair_out.dtype)
+
+    row_tiles(pair_tile)
+    go(small(11, 0, pair_out, far_in, me, far))
+    small(10, 1, products.at[near], near_in.at[0], me, near).wait_recv()
+    small(11, 0, pair_out, far_in, me, far).wait_recv()
+
+    def sum_tile(at):
+        both = products[mine, :, at].astype(jnp.float32) + near_in[0, :, at].astype(jnp.float32)
+        block_out[:, at] = (both + far_in[:, at].astype(jnp.float32)).astype(block_out.dtype)
+
+    row_tiles(sum_tile)
+    last = small(12, 0, block_out, block_in, mine, me)
+
+    @pl.when(jnp.logical_not(on_diagonal))
+    def _():
+        last.start()
+        last.wait()
+        grad_tokens_ref[...] = block_in[...]
+
+    @pl.when(on_diagonal)
+    def _():
+        grad_tokens_ref[...] = block_out[...]
+
+    for block in range(n):
+        itself = jnp.logical_and(on_diagonal, me == block)
+        pl.when(jnp.logical_not(itself))(lambda block=block: grad_copy(block).wait_send())
+
     for way in (0, 1):
 
         @pl.when(ways[way][2])
@@ -322,6 +414,7 @@
     n = lax.axis_size("dp")
     count, cols = cotangent.shape
     depth = w_up.shape[0]
+    down_rows = w_down.shape[0]
     chunks = 4
     tile = 384 if cols % 384 == 0 else 128
     vmem = pl.BlockSpec(memory_space=pltpu.VMEM)
@@ -330,13 +423,24 @@
         functools.partial(exchange_kernel, n, chunks, tile),
         out_shape=(
             jax.ShapeDtypeStruct((count, cols), bf16),
-            jax.ShapeDtypeStruct((n, count, depth), bf16),
-            jax.ShapeDtypeStruct((count, depth), jnp.float32),
-            jax.ShapeDtypeStruct((count, 128), jnp.float32),
+            jax.ShapeDtypeStruct((count, down_rows), bf16),
         ),
         in_specs=[vmem] * 6,
-        out_specs=(vmem,) * 4,
+        out_specs=(vmem,) * 2,
         scratch_shapes=[
+            pltpu.VMEM((count, depth), jnp.float32),
+            pltpu.VMEM((count, 128), jnp.float32),
+            pltpu.VMEM((n, count, depth), bf16),
+            pltpu.VMEM((n, count, depth), bf16),
+            pltpu.VMEM((n, count, depth), bf16),
+            pltpu.VMEM((n, count, down_rows), bf16),
+            pltpu.VMEM((2, count, down_rows), bf16),
+            pltpu.VMEM((count, down_rows), bf16),
+            pltpu.VMEM((count, down_rows), bf16),
+            pltpu.VMEM((count, down_rows), bf16),
+            pltpu.VMEM((count, down_rows), bf16),
+            pltpu.VMEM((count, 128), jnp.float32),
+            pltpu.VMEM((n - 1, count, 128), jnp.float32),
             pltpu.VMEM((depth, cols), bf16),
             pltpu.VMEM((n, count, cols), bf16),
             pltpu.VMEM((2, n, count, cols), bf16),
@@ -351,8 +455,8 @@
             pltpu.VMEM((n - 1, count, 128), jnp.float32),
             pltpu.VMEM((count, depth), bf16),
             pltpu.VMEM((n * count, depth), bf16),
-            pltpu.SemaphoreType.DMA((7, n)),
-            pltpu.SemaphoreType.DMA((7, n)),
+            pltpu.SemaphoreType.DMA((13, n)),
+            pltpu.SemaphoreType.DMA((13, n)),
         ],
         compiler_params=pltpu.CompilerParams(
             collective_id=0, has_side_effects=True, vmem_limit_bytes=60 * 2**20
@@ -361,33 +465,8 @@
 
 
 def move_tokens_body(tokens, w_down, gain, w_up, head_counts, cotangent):
-    n = lax.axis_size("mp")
-    swap = [(i * n + j, j * n + i) for i in range(n) for j in range(n)]
-    latent_width = w_down.shape[1] * n
-    keep_mask = keep_mask_of(head_counts, w_up.shape[1])
-
-    def transpose_owner(block):
-        return lax.ppermute(block, ("dp", "mp"), swap)
-
-    keep_row = keep_mask.astype(jnp.bfloat16)[None, :]
-    queries, grad_partial, latent_raw, root_mean = exchange(
-        tokens, w_down, gain[None, :], w_up, keep_row, cotangent
-    )
-    root_mean = root_mean[:, :1]
-    grad_partial = grad_partial.reshape(-1, grad_partial.shape[-1])
-    grad_latent = transpose_owner(
-        lax.psum_scatter(grad_partial, "mp", scatter_dimension=0, tiled=True)
-    ).astype(jnp.float32)
-    inner_dot = lax.psum(jnp.sum(gain * grad_latent * latent_raw, axis=1, keepdims=True), "mp")
-    grad_raw = (
-        gain * grad_latent / root_mean - latent_raw * inner_dot / (latent_width * root_mean**3)
-    ).astype(jnp.bfloat16)
-    grad_raw_all = lax.all_gather(grad_raw, "dp", axis=0, tiled=True)
-    token_partial = contract_last(grad_raw_all, w_down).astype(jnp.bfloat16)
-    grad_tokens = transpose_owner(
-        lax.psum_scatter(token_partial, "mp", scatter_dimension=0, tiled=True)
-    )
-    return (queries, grad_tokens)
+    keep_row = keep_mask_of(head_counts, w_up.shape[1]).astype(jnp.bfloat16)[None, :]
+    return exchange(tokens, w_down, gain[None, :], w_up, keep_row, cotangent)
 
 
 def solution(mesh):

time: 334 us -> 264 us (0.79)
  waiting for transfers between devices: 75.9 us -> 0 us
  Pallas kernels: 201 us -> 256 us
  blocking collectives: 20.6 us -> 0 us
  between operations: 14.1 us -> 0.65 us
  starting transfers between devices: 10.9 us -> 0 us
    pallas_call x1, Pallas kernels: 201 us -> 256 us  [exchange(): pl.pallas_call(functools.partial(exchange_kernel, n, chunks, tile), out_s...]
    reduce_scatter x2 -> x0, waiting for transfers between devices: 49.6 us -> none  [the longest x1 29.5 us: move_tokens_body(): lax.psum_scatter(token_partial, 'mp', scatter_dimension=0, tiled=True)]
    ppermute x2 -> x0, waiting for transfers between devices: 26.3 us -> none  [transpose_owner(): return lax.ppermute(block, ('dp', 'mp'), swap)]
    all_gather x1 -> x0, blocking collectives: 14.8 us -> none  [move_tokens_body(): grad_raw_all = lax.all_gather(grad_raw, 'dp', axis=0, tiled=True)]
    ppermute x2 -> x0, starting transfers between devices: 10.8 us -> none  [transpose_owner(): return lax.ppermute(block, ('dp', 'mp'), swap)]
    psum x1 -> x0, blocking collectives: 5.77 us -> none  [move_tokens_body(): lax.psum(jnp.sum(gain * grad_latent * latent_raw, axis=1, keepdims=True),...]
  transfers between devices with their start and end apart: 4 -> 0, of which waited for: 4 -> 0; matrix products, arithmetic and copies ran while one was open for 0% -> 0% of each run, Pallas kernels for 0% -> 0%
where the time goes in v4:
time: 264 us
  Pallas kernels  256 us (97%)
  local copies, waits for them, and re-layouts  6.07 us (2%)
    pallas_call x1, Pallas kernels, exchange(): pl.pallas_call(functools.partial(exchange_kernel, n, chunks, tile), out_s...  256 us

profile of v4, /device:TPU:2, one launch (start us, length us, event | category | flops | bytes accessed | tf_op | source)
XLA Modules:
  0.0 264.2 jit_solution(11596607317252935650)
XLA Ops:
  0.6 1.3 dynamic_slice.3
  1.9 1.2 broadcast_in_dim.4.gain_ref
  3.1 1.3 fusion.keep_ref
  4.4 256.1 %shard_map.77 = (bf16[128,6528]{1,0:T(8,128)(2,1)}, bf16[128,1792]{1,0:T(8,128)(2,1)}) custom-call(bf16[128,7168]{1,0:T(8,128)(2,1)} %tokens_ref.1, bf16[1792,384]{1,0:T(8,128)(2,1)} %down_ref.1, f32[1,384]{1,0:T(1,128)} %broadcast_in_dim.4.gain_ref, bf16[384,6528]{1,0:T(8,128)(2,1)} %w_ref.1, bf16[1,6528]{1,0:T(2,128)(2,1)} %fusion.keep_ref, ...), custom_call_target="tpu_custom_call" | custom-call | tf_op jit(solution)/shard_map/pallas_call | solution.py:422
  260.6 0.0 copy-start
  260.6 2.8 %copy.10 = bf16[128,6528]{1,0:T(8,128)(2,1)} copy(bf16[128,6528]{1,0:T(8,128)(2,1)} %get-tuple-element.4) | data formatting | bytes 3342336
  263.4 0.0 copy-done
  263.4 0.8 copy.11
Async XLA Ops:
  260.6 2.8 %copy-start = (bf16[128,1792]{1,0:T(8,128)(2,1)S(1)}, bf16[128,1792]{1,0:T(8,128)(2,1)}, u32[]{:S(2)}) copy-start(bf16[128,1792]{1,0:T(8,128)(2,1)} %get-tuple-element.5) | copy-start | bytes 1376260
